TPU v7x, 32 devices: a whole 2x2x4 slice. The times are simulated.
32 devices in a mesh: gx: 8 (over z, x), gy: 4 (over y, core).
Axes of the slice: x: 2, y: 2, z: 4, core: 2. Of those that a mesh axis runs over, the one named last changes fastest.
Arguments:
- measures: bfloat16 [262144, 128], P(('gx', 'gy')), may hold values from -6 to 6
- row_keys: int32 [262144], P(('gx', 'gy')), may hold values from 0 to 16383, as said below
- orders: bfloat16 [16384, 128], P(('gx', 'gy')), may hold values from -6 to 6
- heavy_keys: int32 [64], replicated, may hold values from 0 to 16383, as said below
- key_slot: int32 [16384], replicated, may hold values from 0 to 16383, as said below
Outputs:
- result: bfloat16 [16384, 128], P(('gx', 'gy'))
- heavy_report: bfloat16 [64, 128], P(('gx', 'gy'))
- slot_rows: float32 [16384], P(('gx', 'gy'))
Inputs may be any that keep to these rules, and one draw needn't show every extreme that they name: `heavy_keys`: for each range block d, entries d * 2 to (d + 1) * 2 - 1 are distinct keys of d * 512 to (d + 1) * 512 - 1. `key_slot`: A permutation. Slot s belongs to owner s // 2048 and to quarter (s // 512) % q with q = 4. Key k lies in range block d = k // 512; every range block has exactly 64 keys with slots of each owner, all in quarter d % q. `row_keys`: in the rows of one device, among rows whose key is not heavy, at most 768 have slots of any one owner and at most 192 distinct keys have slots of any one owner; in every device both bounds are reached by some owner.
All inputs are finite; a program needn't handle non-finite values.
Results may differ from a plain program's by a relative error of at most 0.0021.
Values may be sent and summed in bfloat16 or wider, within the bound.
A program may use at most 64 MiB of HBM per device.

v0:
```python
import jax
import jax.numpy as jnp
from jax import lax
from jax.sharding import PartitionSpec as P


def block_length(total):
    return 2048 if total % 2048 == 0 else total


def one_hot_sums(values, targets, labels, weights):
    block_rows = block_length(targets.shape[0])
    blocks = targets.shape[0] // block_rows
    columns = values.shape[1]
    span = labels.shape[0]
    exact = values.dtype == jnp.float32

    def add_block(running, block_piece):
        block_values, block_targets, block_weights = block_piece
        matches = block_targets[:, None] == labels[None, :]
        onehot = matches.astype(values.dtype)
        if exact:
            product = lax.dot_general(
                onehot,
                block_values,
                (((0,), (0,)), ((), ())),
                precision=lax.Precision.HIGHEST,
                preferred_element_type=jnp.float32,
            )
        else:
            product = lax.dot_general(
                onehot, block_values, (((0,), (0,)), ((), ())), preferred_element_type=jnp.float32
            )
        totals = running[0] + product
        tallies = running[1] + jnp.sum(matches.astype(jnp.float32) * block_weights[:, None], axis=0)
        return ((totals, tallies), jnp.any(matches, axis=1))

    start_state = (jnp.zeros((span, columns), jnp.float32), jnp.zeros((span,), jnp.float32))
    pieces = (
        values.reshape(blocks, block_rows, columns),
        targets.reshape(blocks, block_rows),
        weights.reshape(blocks, block_rows),
    )
    (totals, tallies), matched = lax.scan(add_block, start_state, pieces)
    return (totals, tallies, matched.reshape(-1))


def body(measures, row_keys, orders, heavy_keys, key_slot):
    row_count, columns = measures.shape
    groups_x = lax.axis_size("gx")
    groups_y = lax.axis_size("gy")
    key_dev = orders.shape[0]
    own_slots = key_dev * groups_y
    heavy_total = heavy_keys.shape[0]
    heavy_each = heavy_total // (groups_x * groups_y)
    capacity = max(row_count // 32, 3 * row_count // (4 * groups_x))
    key_capacity = capacity // 4
    index_x = lax.axis_index("gx")
    index_y = lax.axis_index("gy")
    device = index_x * groups_y + index_y
    unit_rows = jnp.ones((row_count,), jnp.float32)
    heavy_part, heavy_count, heavy_flags = one_hot_sums(measures, row_keys, heavy_keys, unit_rows)
    slot_ids = key_slot[row_keys]
    owner_labels = jnp.arange(groups_x + 1, dtype=jnp.int32)
    own_base = index_x * own_slots
    own_labels = jnp.arange(own_slots, dtype=jnp.int32)
    sort_keys = jnp.where(heavy_flags, groups_x * own_slots, slot_ids)
    ordering = jnp.argsort(sort_keys, stable=True)
    sorted_slots = sort_keys[ordering]
    sorted_owner = sorted_slots // own_slots
    is_light = sorted_owner < groups_x
    fresh = (
        jnp.concatenate([jnp.ones((1,), bool), sorted_slots[1:] != sorted_slots[:-1]]) & is_light
    )
    distinct = jnp.cumsum(fresh.astype(jnp.int32)) - 1
    before = jnp.sum(
        (fresh[:, None] & (sorted_owner[:, None] < owner_labels[None, :])).astype(jnp.int32), axis=0
    )
    segments = groups_x * key_capacity
    segment = jnp.where(
        is_light, sorted_owner * key_capacity + distinct - before[sorted_owner], segments
    )
    row_segment = jnp.zeros((row_count,), jnp.int32).at[ordering].set(segment)
    partial_value, tallies, unused = one_hot_sums(
        measures, row_segment, jnp.arange(segments, dtype=jnp.int32), unit_rows
    )
    sent_slots = jnp.full((segments + 1,), -1, jnp.int32).at[segment].set(sorted_slots)[:segments]
    got_sums, got_tallies, got_slots = (
        lax.all_to_all(
            partial_value.reshape(groups_x, key_capacity, columns),
            "gx",
            split_axis=0,
            concat_axis=0,
            tiled=True,
        ),
        lax.all_to_all(
            tallies.reshape(groups_x, key_capacity), "gx", split_axis=0, concat_axis=0, tiled=True
        ),
        lax.all_to_all(
            sent_slots.reshape(groups_x, key_capacity),
            "gx",
            split_axis=0,
            concat_axis=0,
            tiled=True,
        ),
    )
    local_slot = got_slots.reshape(-1) - own_base
    local_slot = jnp.where(got_slots.reshape(-1) >= 0, local_slot, own_slots)
    light_totals, light_tallies, unused_too = one_hot_sums(
        got_sums.reshape(-1, columns), local_slot, own_labels, got_tallies.reshape(-1)
    )
    quarter_totals, quarter_tallies = (
        lax.psum_scatter(
            light_totals.reshape(groups_y, key_dev, columns), "gy", scatter_dimension=0, tiled=True
        ),
        lax.psum_scatter(
            light_tallies.reshape(groups_y, key_dev), "gy", scatter_dimension=0, tiled=True
        ),
    )
    slot_rows = quarter_tallies.reshape(key_dev)
    inverse = jnp.argsort(key_slot)
    held_keys = lax.dynamic_slice_in_dim(inverse, device * key_dev, key_dev)
    send_order = jnp.argsort(held_keys)
    per_peer = key_dev // groups_x
    moved_totals, moved_tallies = (
        lax.all_to_all(
            quarter_totals.reshape(key_dev, columns)[send_order].reshape(
                groups_x, per_peer, columns
            ),
            "gx",
            split_axis=0,
            concat_axis=0,
            tiled=True,
        ),
        lax.all_to_all(
            slot_rows[send_order].reshape(groups_x, per_peer),
            "gx",
            split_axis=0,
            concat_axis=0,
            tiled=True,
        ),
    )
    range_slots = lax.dynamic_slice_in_dim(key_slot, device * key_dev, key_dev)
    arrival = jnp.argsort(range_slots // own_slots, stable=True)
    placed = jnp.argsort(arrival)
    light_sum = moved_totals.reshape(key_dev, columns)[placed]
    light_count = moved_tallies.reshape(key_dev)[placed]
    my_heavy = lax.dynamic_slice_in_dim(heavy_keys, device * heavy_each, heavy_each)
    heavy_local = my_heavy - device * key_dev
    heavy_orders_here = orders[heavy_local]
    gathered = lax.all_gather(heavy_orders_here, ("gx", "gy"), axis=0, tiled=True)
    joined = heavy_part * gathered.astype(jnp.float32)
    joined_total, count_total = lax.psum((joined, heavy_count), ("gx", "gy"))
    mine_joined = lax.dynamic_slice_in_dim(joined_total, device * heavy_each, heavy_each)
    mine_count = lax.dynamic_slice_in_dim(count_total, device * heavy_each, heavy_each)
    heavy_value = mine_joined * lax.rsqrt(1.0 + mine_count)[:, None]
    light_value = orders.astype(jnp.float32) * light_sum * lax.rsqrt(1.0 + light_count)[:, None]
    placing = (heavy_local[:, None] == jnp.arange(key_dev, dtype=jnp.int32)[None, :]).astype(
        jnp.float32
    )
    heavy_full = jnp.sum(placing[:, :, None] * heavy_value[:, None, :], axis=0)
    result = (light_value + heavy_full).astype(jnp.bfloat16)
    return (result, heavy_value.astype(jnp.bfloat16), slot_rows)


def solution(mesh):
    return jax.shard_map(
        body,
        mesh=mesh,
        in_specs=(P(("gx", "gy"), None), P(("gx", "gy")), P(("gx", "gy"), None), P(), P()),
        out_specs=(P(("gx", "gy"), None), P(("gx", "gy"), None), P(("gx", "gy"))),
        check_vma=False,
    )
```

profile of v0, /device:TPU:15, one launch (start us, length us, event | category | flops | bytes accessed | tf_op | source)
XLA Modules:
  0.0 401.7 jit_solution(12164380390125514987)
XLA Ops:
  7.2 0.8 reshape.279
  8.0 0.8 fusion.26
  8.8 12.8 %while.33 = (s32[]{:T(128)}, f32[64,128]{1,0:T(8,128)S(1)}, f32[64]{0:T(128)S(1)}, pred[4,2048]{1,0:T(4,128)(4,1)S(1)}, s32[4,2048]{1,0:T(4,128)S(1)}, /*index=5...) while((s32[]{:T(128)}, f32[64,128]{1,0:T(8,128)S(1)}, f32[64]{0:T(128)S(1)}, ...), condition=%wide.region_3.4_spmd.clone, body=%wide.region_0.3_spmd.clone.sunk | while | flops 34355264 | bytes 643696 | solution.py:44
  8.8 1.3 convolution_add_fusion.2
  10.1 0.9 fusion.53
  11.0 0.8 compare_reduce_fusion.4
  12.0 1.3 convolution_add_fusion.2
  13.3 0.9 fusion.53
  14.2 0.8 compare_reduce_fusion.4
  15.2 1.3 convolution_add_fusion.2
  16.5 0.9 fusion.53
  17.4 0.8 compare_reduce_fusion.4
  18.4 1.3 convolution_add_fusion.2
  19.7 0.9 fusion.53
  20.6 0.8 compare_reduce_fusion.4
  21.6 45.5 %gather_fusion = s32[8192]{0:T(1024)S(1)} fusion(s32[16384]{0:T(1024)S(1)} %copy-done, s32[8192]{0:T(1024)S(1)} %fusion.26), kind=kCustom, calls=%fused_computation | custom fusion | bytes 98304 | tf_op jit(solution)/shard_map/gather | solution.py:63
  67.2 6.8 %sort.82 = (s32[8192]{0:T(1024)}, s32[8192]{0:T(1024)S(1)}) sort(s32[8192]{0:T(1024)S(1)} %broadcast_select_fusion.1, s32[8192]{0:T(1024)S(1)} %iota.43), dimensions={0}, to_apply=%region_4.5 | sort | flops 106496 | bytes 131072 | tf_op jit(solution)/shard_map/jit(argsort)/sort | solution.py:68
  73.9 45.5 %gather_fusion.1 = s32[8192]{0:T(1024)S(1)} fusion(s32[8192]{0:T(1024)S(1)} %broadcast_select_fusion.1, s32[8192]{0:T(1024)S(1)} %get-tuple-element.195), kind=kCustom, calls=%fused_computation.1 | custom fusion | bytes 98304 | tf_op jit(solution)/shard_map/gather | solution.py:69
  119.7 0.2 convert_reduce_fusion
  119.9 0.7 fusion.42
  120.6 4.7 %compare_select_fusion.3 = (s32[8192,1]{0,1:T(1,128)S(1)}, s32[8192,1]{0,1:T(1,128)S(1)}, s32[8192,1]{0,1:T(1,128)S(1)}) fusion(s32[]{:T(128)} %bitcast.7, s32[]{:T(128)} %bitcast.8, s32[]{:T(128)} %bitcast.9, s32[]{:T(128)} %bitcast.10, s32[]{:T(128)} %bitcast.11, s32[]{:T(128)} %bitcast.13, s32[]{:T(128)} %bitcast.12, s32[8192,1]{0,1:T(1,128)S(1)} %bitcast.83), kind=kLoop, calls=%fused_computation.49 | loop fusion | flops 245760 | bytes 131100 | tf_op jit(solution)/shard_map/gather | solution.py:81
  125.5 0.3 reduce-window.9
  126.1 1.4 fusion.28
  127.5 30.4 %scatter_custom_fusion = s32[1537]{0:T(1024)S(1)} fusion(s32[8192]{0:T(1024)S(1)} %bitcast.93, s32[8192]{0:T(1024)S(1)} %gather_fusion.1, s32[]{:T(128)} %constant.66.clone.1), kind=kCustom, calls=%fused_computation.106 | custom fusion | bytes 6152 | tf_op jit(solution)/shard_map/scatter | solution.py:87
  158.0 0.7 all_to_all.24
  158.7 5.7 %all-to-all-start = ((s32[8,1,192]{2,1,0:T(1,128)}), s32[8,1,192]{2,1,0:T(1,128)S(1)}, u32[]{:S(2)}, u32[]{:S(2)}) async-start(s32[8,1,192]{2,1,0:T(1,128)} %all_to_all.24), calls=%async_computation | async-start | bytes 16384 | tf_op jit(solution)/shard_map/all_to_all | solution.py:99
  164.3 30.7 %scatter_custom_fusion.1 = s32[8192]{0:T(1024)S(1)} fusion(s32[8192]{0:T(1024)S(1)} %get-tuple-element.196, s32[8192]{0:T(1024)S(1)} %get-tuple-element.185, s32[]{:T(128)} %constant.68.clone.1), kind=kCustom, calls=%fused_computation.95 | custom fusion | bytes 32772 | tf_op jit(solution)/shard_map/scatter | solution.py:83
  195.0 30.3 %while.34 = (s32[]{:T(128)}, f32[1536,128]{1,0:T(8,128)}, f32[1536]{0:T(1024)S(1)}, s32[4,2048]{1,0:T(4,128)S(1)}, bf16[4,2048,128]{2,1,0:T(8,128)(2,1)}, /*index=5*/s32[]{:T(128)}, s32[]{:T(128)}) while((s32[]{:T(128)}, f32[1536,128]{1,0:T(8,128)}, f32[1536]{0:T(1024)S(1)}, s32[4,2048]{1,0:T(4,128)S(1)}, ...), condition=%wide.region_12.13_spmd.clone, body=%wide.region_10.12_spmd.clone.sunk | while | flops 818284032 | bytes 2155100 | solution.py:44
  195.0 5.7 %fusion.56 = f32[1536,128]{1,0:T(8,128)} fusion(s32[2048]{0:T(1024)S(1)} %bitcast.85, f32[1536,128]{1,0:T(8,128)} %get-tuple-element.315, bf16[4,2048,128]{2,1,0:T(8,128)(2,1)} %get-tuple-element.325, s32[]{:T(128)} %get-tuple-element.314, pred[]{:T(512)S(6)} %compare.110), kind=kOutput, calls=%fused_computation.28.clone.1 | convolution fusion | flops 808845312 | bytes 2105857 | tf_op jit(solution)/shard_map/while/body/eval_jaxpr/dot_general | solution.py:31
  200.7 1.7 fusion.57
  202.4 5.9 %fusion.56 = f32[1536,128]{1,0:T(8,128)} fusion(s32[2048]{0:T(1024)S(1)} %bitcast.85, f32[1536,128]{1,0:T(8,128)} %get-tuple-element.315, bf16[4,2048,128]{2,1,0:T(8,128)(2,1)} %get-tuple-element.325, s32[]{:T(128)} %get-tuple-element.314, pred[]{:T(512)S(6)} %compare.110), kind=kOutput, calls=%fused_computation.28.clone.1 | convolution fusion | flops 808845312 | bytes 2105857 | tf_op jit(solution)/shard_map/while/body/eval_jaxpr/dot_general | solution.py:31
  208.3 1.7 fusion.57
  210.1 5.9 %fusion.56 = f32[1536,128]{1,0:T(8,128)} fusion(s32[2048]{0:T(1024)S(1)} %bitcast.85, f32[1536,128]{1,0:T(8,128)} %get-tuple-element.315, bf16[4,2048,128]{2,1,0:T(8,128)(2,1)} %get-tuple-element.325, s32[]{:T(128)} %get-tuple-element.314, pred[]{:T(512)S(6)} %compare.110), kind=kOutput, calls=%fused_computation.28.clone.1 | convolution fusion | flops 808845312 | bytes 2105857 | tf_op jit(solution)/shard_map/while/body/eval_jaxpr/dot_general | solution.py:31
  216.0 1.7 fusion.57
  217.7 5.9 %fusion.56 = f32[1536,128]{1,0:T(8,128)} fusion(s32[2048]{0:T(1024)S(1)} %bitcast.85, f32[1536,128]{1,0:T(8,128)} %get-tuple-element.315, bf16[4,2048,128]{2,1,0:T(8,128)(2,1)} %get-tuple-element.325, s32[]{:T(128)} %get-tuple-element.314, pred[]{:T(512)S(6)} %compare.110), kind=kOutput, calls=%fused_computation.28.clone.1 | convolution fusion | flops 808845312 | bytes 2105857 | tf_op jit(solution)/shard_map/while/body/eval_jaxpr/dot_general | solution.py:31
  223.6 1.7 fusion.57
  225.3 5.4 %all-to-all-start.1 = ((f32[8,192,128]{2,1,0:T(8,128)}), f32[8,192,128]{2,1,0:T(8,128)S(1)}, u32[]{:S(2)}, u32[]{:S(2)}) async-start(f32[8,192,128]{2,1,0:T(8,128)} %bitcast.18), calls=%async_computation.1 | async-start | bytes 1572864 | tf_op jit(solution)/shard_map/all_to_all | solution.py:89
  230.9 17.4 %all-to-all-done.1 = f32[8,192,128]{2,1,0:T(8,128)S(1)} async-done(((f32[8,192,128]{2,1,0:T(8,128)}), f32[8,192,128]{2,1,0:T(8,128)S(1)}, u32[]{:S(2)}, u32[]{:S(2)}) %all-to-all-start.1) | async-done | bytes 786464 | tf_op jit(solution)/shard_map/all_to_all | solution.py:89
  248.3 6.3 %fusion.18 = f32[4,512,128]{2,1,0:T(8,128)} fusion(f32[1536,128,1]{1,0,2:T(8,128)S(1)} %bitcast.84, s32[4,512]{1,0:T(4,128)S(1)} %multiply_add_fusion, s32[1536]{0:T(1024)S(1)} %select_n.113), kind=kOutput, calls=%fused_computation.36 | convolution fusion | flops 4834983936 | bytes 1849344 | tf_op jit(solution)/shard_map/while/body/eval_jaxpr/dot_general | solution.py:23
  254.6 0.7 all_to_all.28
  255.3 6.4 %all-to-all-start.3 = ((f32[8,1,192]{2,1,0:T(1,128)}), f32[8,1,192]{2,1,0:T(1,128)S(1)}, u32[]{:S(2)}, u32[]{:S(2)}) async-start(f32[8,1,192]{2,1,0:T(1,128)} %all_to_all.28), calls=%async_computation.4 | async-start | bytes 16384 | tf_op jit(solution)/shard_map/all_to_all | solution.py:96
  261.7 7.8 %sort.83 = (s32[16384]{0:T(1024)}, s32[16384]{0:T(1024)S(1)}) sort(s32[16384]{0:T(1024)S(1)} %copy-done, s32[16384]{0:T(1024)S(1)} %iota.45), dimensions={0}, to_apply=%region_14.15 | sort | flops 229376 | bytes 262144 | tf_op jit(solution)/shard_map/jit(argsort)/sort | solution.py:121
  269.4 0.6 dynamic-slice.1
  270.1 3.8 sort.84
  273.9 3.8 sort.85
  277.7 3.8 sort.86
  281.6 0.6 gather_fusion.6
  282.1 29.6 %all-gather.1 = bf16[32,2,128]{2,1,0:T(2,128)(2,1)S(1)} all-gather(bf16[1,2,128]{2,1,0:T(2,128)(2,1)S(1)} %bitcast.95), channel_id=2, replica_groups=mesh['gx'=8,'gy'=4] {'gx','gy'}, dimensions={0}, use_global_device_ids=true | all-gather | bytes 16896 | tf_op jit(solution)/shard_map/all_gather | solution.py:151
  311.9 49.8 %all-reduce.1 = (f32[64,128]{1,0:T(8,128)S(1)}, f32[64]{0:T(128)S(1)}) all-reduce(f32[64,128]{1,0:T(8,128)S(1)} %convert_multiply_fusion, f32[64]{0:T(128)S(1)} %get-tuple-element.110), channel_id=1, replica_groups=mesh['gx'=8,'gy'=4] {'gx','gy'}, use_global_device_ids=true, to_apply=%region_20.21 | all-reduce | flops 8256 | bytes 66048 | tf_op jit(solution)/shard_map/psum | solution.py:153
  361.8 1.8 select_reduce_fusion
  363.6 6.3 %all-reduce = f32[4,512]{1,0:T(4,128)S(1)} all-reduce(f32[4,512]{1,0:T(4,128)S(1)} %reshape.288), channel_id=4, replica_groups=mesh['gx'=8,'gy'=4] {'gy'}, use_global_device_ids=true, to_apply=%region_19.20.clone | all-reduce | flops 2048 | bytes 16384
  370.0 0.7 constant_dynamic-slice_fusion.2
  370.6 3.5 gather_fusion.4
  374.1 0.7 all_to_all.30
  374.8 3.9 all-to-all-start.4
  378.8 2.6 gather_fusion.2
  381.4 0.5 all-to-all-done.4
  382.0 5.4 %all-to-all-start.2 = ((f32[8,64,128]{2,1,0:T(8,128)}), f32[8,64,128]{2,1,0:T(8,128)S(1)}, u32[]{:S(2)}, u32[]{:S(2)}) async-start(f32[8,64,128]{2,1,0:T(8,128)} %bitcast.22), calls=%async_computation.3 | async-start | bytes 524288 | tf_op jit(solution)/shard_map/all_to_all | solution.py:126
  387.4 0.6 fusion.41
  388.1 0.5 broadcast.477
  388.7 0.7 reduce.12
  389.4 3.5 gather_fusion.5
  393.0 1.0 gather_fusion.3
  394.1 0.8 add_convert_fusion
  (82 shorter events, 2.4 us)
Async XLA Ops:
  7.2 14.4 %copy-start = (s32[16384]{0:T(1024)S(1)}, s32[16384]{0:T(1024)}, u32[]{:S(2)}) copy-start(s32[16384]{0:T(1024)} %param.13) | copy-start | bytes 196612
  158.7 66.6 %all-to-all-start = ((s32[8,1,192]{2,1,0:T(1,128)}), s32[8,1,192]{2,1,0:T(1,128)S(1)}, u32[]{:S(2)}, u32[]{:S(2)}) async-start(s32[8,1,192]{2,1,0:T(1,128)} %all_to_all.24), calls=%async_computation | async-start | bytes 16384 | tf_op jit(solution)/shard_map/all_to_all | solution.py:99
  225.3 23.0 %all-to-all-start.1 = ((f32[8,192,128]{2,1,0:T(8,128)}), f32[8,192,128]{2,1,0:T(8,128)S(1)}, u32[]{:S(2)}, u32[]{:S(2)}) async-start(f32[8,192,128]{2,1,0:T(8,128)} %bitcast.18), calls=%async_computation.1 | async-start | bytes 1572864 | tf_op jit(solution)/shard_map/all_to_all | solution.py:89
  230.7 148.1 %reduce-scatter.2.cloned.1.call-start = ((), (), s32[]{:S(2)}) async-start(), calls=%async_computation.6 | async-start | bytes 1310720 | tf_op jit(solution)/shard_map/reduce_scatter | solution.py:113
  248.3 21.1 %copy-start.4 = (u32[32]{0:T(128)S(1)}, u32[32]{0:T(128)}, u32[]{:S(2)}) copy-start(u32[32]{0:T(128)} %constant.146) | copy-start | bytes 388
  248.3 33.2 %copy-start.3 = (s32[64]{0:T(128)S(1)}, s32[64]{0:T(128)}, u32[]{:S(2)}) copy-start(s32[64]{0:T(128)} %get-tuple-element.335) | copy-start | bytes 772
  248.3 33.2 %copy-start.2 = (bf16[512,128]{1,0:T(8,128)(2,1)S(1)}, bf16[512,128]{1,0:T(8,128)(2,1)}, u32[]{:S(2)}) copy-start(bf16[512,128]{1,0:T(8,128)(2,1)} %param.11) | copy-start | bytes 393220
  255.3 106.4 %all-to-all-start.3 = ((f32[8,1,192]{2,1,0:T(1,128)}), f32[8,1,192]{2,1,0:T(1,128)S(1)}, u32[]{:S(2)}, u32[]{:S(2)}) async-start(f32[8,1,192]{2,1,0:T(1,128)} %all_to_all.28), calls=%async_computation.4 | async-start | bytes 16384 | tf_op jit(solution)/shard_map/all_to_all | solution.py:96
  370.6 10.8 %copy-start.1 = (f32[1,512]{1,0:T(1,128)}, f32[1,512]{1,0:T(1,128)S(1)}, u32[]{:S(2)}) copy-start(f32[1,512]{1,0:T(1,128)S(1)} %constant_dynamic-slice_fusion.2) | copy-start | bytes 6148
  374.8 7.1 %all-to-all-start.4 = ((f32[8,1,64]{2,1,0:T(1,128)}), f32[8,1,64]{2,1,0:T(1,128)S(1)}, u32[]{:S(2)}, u32[]{:S(2)}) async-start(f32[8,1,64]{2,1,0:T(1,128)} %all_to_all.30), calls=%async_computation.5 | async-start | bytes 8192 | tf_op jit(solution)/shard_map/all_to_all | solution.py:135
  382.0 11.1 %all-to-all-start.2 = ((f32[8,64,128]{2,1,0:T(8,128)}), f32[8,64,128]{2,1,0:T(8,128)S(1)}, u32[]{:S(2)}, u32[]{:S(2)}) async-start(f32[8,64,128]{2,1,0:T(8,128)} %bitcast.22), calls=%async_computation.3 | async-start | bytes 524288 | tf_op jit(solution)/shard_map/all_to_all | solution.py:126
Sparse Core Ops, SparseCore 0:
  254.7 25.5 reduce-scatter.1
where the time goes:
time: 409 us; the launch traced here: 402 us
  local copies, waits for them, and re-layouts  170 us (42%)
  blocking collectives  85.8 us (21%)
  other arithmetic  51.7 us (13%)
  matrix products  35 us (9%)
  starting transfers between devices  26.8 us (7%)
  waiting for transfers between devices  18.1 us (4%)
  between operations  14.3 us (3%)
    psum x1, blocking collectives, body(): joined_total, count_total = lax.psum((joined, heavy_count), ('gx', 'gy'))  49.8 us
    gather x1, local copies, waits for them, and re-layouts, body(): slot_ids = key_slot[row_keys]  45.5 us
    gather x1, local copies, waits for them, and re-layouts, body(): sorted_slots = sort_keys[ordering]  45.5 us
    scatter x1, local copies, waits for them, and re-layouts, body(): row_segment = jnp.zeros((row_count,), jnp.int32).at[ordering].set(segment)  30.7 us
    scatter x1, local copies, waits for them, and re-layouts, body(): jnp.full((segments + 1,), -1, jnp.int32).at[segment].set(sorted_slots)  30.4 us
    all_gather x1, blocking collectives, body(): lax.all_gather(heavy_orders_here, ('gx', 'gy'), axis=0, tiled=True)  29.6 us
    dot_general x8, matrix products, add_block(): lax.dot_general(onehot, block_values, (((0,), (0,)), ((), ())), preferred...  28.7 us
    all_to_all x1, waiting for transfers between devices, body(): lax.all_to_all(partial_value.reshape(groups_x, key_capacity, columns), 'g...  17.4 us
  transfers between devices with their start and end apart: 6, of which 3 were waited for; matrix products, arithmetic and copies ran while one was open for 24% of the time, Pallas kernels for 0%

commit v1 on v0

v1 whole, which is shorter than its diff:
```python
import functools

import jax
import jax.numpy as jnp
from jax import lax
from jax.experimental import pallas as pl
from jax.experimental.pallas import tpu as pltpu
from jax.sharding import PartitionSpec as P

MESH = pl.DeviceIdType.MESH
LANES = 128
F32 = jnp.float32
BF16 = jnp.bfloat16
VMEM = pl.BlockSpec(memory_space=pltpu.VMEM)
ANY = pl.BlockSpec(memory_space=pl.ANY)
SMEM = pl.BlockSpec(memory_space=pltpu.SMEM)
LIMIT = 60 * 1024 * 1024
NN = (((1,), (0,)), ((), ()))
NT = (((1,), (1,)), ((), ()))


def dot(a, b, dims=NN):
    return lax.dot_general(a, b, dims, preferred_element_type=F32)


def iota(shape, dim):
    return lax.broadcasted_iota(jnp.int32, shape, dim)


def onehot(mask):
    return jnp.where(mask, 1.0, 0.0).astype(BF16)


def group_rank(flags, group_rows):
    rows = flags.shape[0]
    lane_r, lane_c = iota((LANES, LANES), 0), iota((LANES, LANES), 1)
    inside = dot(flags, onehot(lane_r < lane_c))
    whole = dot(flags, onehot(lane_r >= 0))
    row_r, row_c = iota((rows, rows), 0), iota((rows, rows), 1)
    earlier = onehot((row_c < row_r) & (row_r // group_rows == row_c // group_rows))
    return inside + dot(earlier, whole.astype(BF16))


def split(values):
    high = values.astype(BF16)
    low = (values - high.astype(F32)).astype(BF16)
    return jnp.concatenate([high, low], axis=1)


def byte_table(table, parts):
    pieces = [((table >> (8 * p)) & 255).astype(F32).T for p in range(parts)]
    return jnp.concatenate(pieces, axis=0).astype(BF16)


def look_up(bytes_table, row_hot, column_mask, parts):
    wide = dot(bytes_table, row_hot)
    found = 0.0
    for p in range(parts):
        piece = wide[p * LANES : (p + 1) * LANES]
        found = found + float(256**p) * jnp.sum(
            jnp.where(column_mask, piece, 0.0), axis=0, keepdims=True
        )
    return found.astype(jnp.int32)


def byte_count(largest):
    return (int(largest).bit_length() + 7) // 8


def gather_rows(cfg, measures, keys, heavy, key_slot, send, tally, small, slots):
    rows, block, nr = cfg["rows"], cfg["block"], cfg["nr"]
    segments, capacity = cfg["segments"], cfg["capacity"]
    slot_parts = byte_count(nr * LANES - 1)
    slot_bytes = byte_table(key_slot[...], slot_parts)
    hist_key = jnp.zeros((nr, LANES), F32)
    hist_slot = jnp.zeros((nr, LANES), F32)
    heavy_sum = jnp.zeros((cfg["heavy"], LANES), F32)
    for c in range(rows // block):
        span = slice(c * block, (c + 1) * block)
        key = keys[:, span]
        row_hot = onehot(iota((nr, block), 0) == key >> 7)
        column_mask = iota((LANES, block), 0) == (key & 127)
        hist_key = hist_key + dot(row_hot, onehot(column_mask), NT)
        heavy_hot = jnp.where(heavy[...] == key, 1.0, 0.0)
        is_heavy = jnp.max(heavy_hot, axis=0, keepdims=True) > 0.0
        heavy_sum = heavy_sum + dot(heavy_hot.astype(BF16), measures[span, :])
        slot = jnp.where(is_heavy, -1, look_up(slot_bytes, row_hot, column_mask, slot_parts))
        slots[:, span] = slot
        slot_row = onehot(iota((nr, block), 0) == slot >> 7)
        slot_column = onehot(iota((LANES, block), 0) == (slot & 127))
        hist_slot = hist_slot + dot(slot_row, slot_column, NT)
    tally[...] = hist_slot
    present = hist_slot > 0.0
    group = cfg["own"] // LANES
    rank = group_rank(onehot(present), group).astype(jnp.int32)
    owner = iota((nr, LANES), 0) // group
    segment_table = jnp.where(present, owner * capacity + rank + 1, 0)
    seg_parts = byte_count(segments)
    segment_bytes = byte_table(segment_table, seg_parts)
    step = cfg["seg_block"]
    for c in range(rows // block):
        span = slice(c * block, (c + 1) * block)
        slot = slots[:, span]
        slot_row = onehot(iota((nr, block), 0) == slot >> 7)
        slot_mask = iota((LANES, block), 0) == (slot & 127)
        segment = look_up(segment_bytes, slot_row, slot_mask, seg_parts) - 1
        for s in range(segments // step):
            hot = onehot(iota((step, block), 0) == segment - s * step)
            product = dot(hot, measures[span, :])
            place = slice(s * step, (s + 1) * step)
            if c == 0:
                send[place, :] = product
            else:
                send[place, :] += product
    each, key_rows, height = cfg["heavy_each"], cfg["key_rows"], cfg["height"]
    small[...] = jnp.zeros(small.shape, F32)
    for d in range(cfg["devices"]):
        small[d * height : d * height + each, :] = heavy_sum[d * each : (d + 1) * each]
        top = (d + 1) * height
        small[top - key_rows : top, :] = hist_key[d * key_rows : (d + 1) * key_rows]


def place_rows(cfg, got, got_tally, key_slot, send, tally, spread, ranks):
    gx, gy, own, kpp = cfg["gx"], cfg["gy"], cfg["own"], cfg["kpp"]
    key_rows, capacity = cfg["key_rows"], cfg["capacity"]
    group = own // LANES
    base = lax.axis_index("gx") * own
    local = key_slot[...] - base
    mine = (local >= 0) & (local < own)
    rank = jnp.where(mine, group_rank(onehot(mine), key_rows), -1.0).astype(jnp.int32)
    local = local.astype(F32)
    for y in range(gy):
        for x in range(gx):
            first = (x * gy + y) * key_rows
            acc = jnp.zeros((kpp, LANES), F32)
            for j in range(key_rows):
                hit = iota((kpp, LANES), 0) == rank[first + j : first + j + 1]
                acc = acc + jnp.where(hit, local[first + j : first + j + 1], 0.0)
            at = (y * gx + x) * kpp
            spread[at : at + kpp, :] = acc
    present = got_tally[...] > 0.0
    ranks[...] = jnp.where(present, group_rank(onehot(present), group) + 1.0, 0.0)
    total = got_tally[0:group]
    for i in range(1, gx):
        total = total + got_tally[i * group : (i + 1) * group]
    tally[...] = total
    values = split(got[...])
    quarter = own // gy
    for q in range(gy):
        at = slice(q * quarter, (q + 1) * quarter)
        slot = jnp.sum(spread[at, :], axis=1, keepdims=True).astype(jnp.int32) - q * quarter
        found = jnp.zeros((quarter, gx), F32)
        for j in range(key_rows):
            hot = onehot(slot - j * LANES == iota((quarter, LANES), 1))
            table = ranks[pl.ds(q * key_rows + j, gx, stride=group), :].astype(BF16)
            found = found + dot(hot, table, NT)
        found = found.astype(jnp.int32) - 1
        out = jnp.zeros((quarter, 2 * LANES), F32)
        for i in range(gx):
            hot = onehot(found[:, i : i + 1] == iota((quarter, capacity), 1))
            out = out + dot(hot, values[i * capacity : (i + 1) * capacity])
        send[at, :] = out[:, :LANES] + out[:, LANES:]


def join_rows(cfg, heavy, got, got_small, got_tally, orders, key_slot, result, report, slot_rows, sums, joined):
    gx, gy, own, kpp = cfg["gx"], cfg["gy"], cfg["own"], cfg["kpp"]
    key_rows, height, each = cfg["key_rows"], cfg["height"], cfg["heavy_each"]
    key_dev = key_rows * LANES
    device = lax.axis_index("gx") * gy + lax.axis_index("gy")
    total = got_tally[0:key_rows]
    for y in range(1, gy):
        total = total + got_tally[y * key_rows : (y + 1) * key_rows]
    slot_rows[...] = total
    small = got_small[0:height]
    for d in range(1, cfg["devices"]):
        small = small + got_small[d * height : (d + 1) * height]
    for x in range(gx):
        first = x * gy * kpp
        part = got[first : first + kpp]
        for y in range(1, gy):
            part = part + got[first + y * kpp : first + (y + 1) * kpp]
        sums[x * kpp : (x + 1) * kpp, :] = part
    values = split(sums[...])
    owner = key_slot[pl.ds(device * key_rows, key_rows), :] // own
    flags = jnp.concatenate([jnp.where(owner == x, 1.0, 0.0) for x in range(gx)], axis=0)
    rank = group_rank(flags.astype(BF16), key_rows)
    place = jnp.zeros((key_rows, LANES), F32)
    for x in range(gx):
        here = rank[x * key_rows : (x + 1) * key_rows] + float(x * kpp)
        place = place + jnp.where(owner == x, here, 0.0)
    counts = small[height - key_rows : height]
    stacked = jnp.concatenate([place, counts], axis=0)
    columns = stacked.T
    for j in range(key_rows):
        at = slice(j * LANES, (j + 1) * LANES)
        where = columns[:, j : j + 1].astype(jnp.int32)
        hot = onehot(where == iota((LANES, key_dev), 1))
        both = dot(hot, values)
        found = both[:, :LANES] + both[:, LANES:]
        for h in range(each):
            spot = heavy[device * each + h] - device * key_dev - j * LANES
            found = found + jnp.where(iota((LANES, LANES), 0) == spot, small[h : h + 1], 0.0)
        scale = lax.rsqrt(1.0 + columns[:, key_rows + j : key_rows + j + 1])
        value = orders[at, :].astype(F32) * found * scale
        joined[at, :] = value
        result[at, :] = value.astype(BF16)
    lines = [
        joined[pl.ds(heavy[device * each + h] - device * key_dev, 1), :] for h in range(each)
    ]
    report[...] = jnp.concatenate(lines, axis=0).astype(BF16)


def all_barrier(gx, gy, me_x, me_y):
    barrier = pltpu.get_barrier_semaphore()
    device = me_x * gy + me_y
    devices = gx * gy

    @pl.loop(1, devices)
    def _(step):
        other = lax.rem(device + step, devices)
        target = (other // gy, lax.rem(other, gy))
        pl.semaphore_signal(barrier, inc=1, device_id=target, device_id_type=MESH)

    pl.semaphore_wait(barrier, devices - 1)


def exchange(me, count, moves, address):
    for source, landing, send_sem, recv_sem, local_sem in moves:
        pltpu.make_async_copy(source(me), landing(me), local_sem).start()

    def remote(other, move):
        source, landing, send_sem, recv_sem, local_sem = move
        return pltpu.make_async_remote_copy(
            src_ref=source(other),
            dst_ref=landing(me),
            send_sem=send_sem.at[other],
            recv_sem=recv_sem.at[me],
            device_id=address(other),
            device_id_type=MESH,
        )

    def finish(other, move):
        source, landing, send_sem, recv_sem, local_sem = move
        copy = pltpu.make_async_remote_copy(
            src_ref=source(other),
            dst_ref=landing(other),
            send_sem=send_sem.at[other],
            recv_sem=recv_sem.at[other],
            device_id=address(other),
            device_id_type=MESH,
        )
        copy.wait_send()
        copy.wait_recv()

    @pl.loop(1, count)
    def _(step):
        for move in moves:
            remote(lax.rem(me + step, count), move).start()

    def end():
        @pl.loop(1, count)
        def _(step):
            for move in moves:
                finish(lax.rem(me + step, count), move)

        for source, landing, send_sem, recv_sem, local_sem in moves:
            pltpu.make_async_copy(source(me), landing(me), local_sem).wait()

    return end


def to_owners(gx, gy, send, tally, small, got, got_tally, got_small, sem_a, sem_b, sem_c, sem_d, sem_e, sem_f, local):
    me_x, me_y = lax.axis_index("gx"), lax.axis_index("gy")
    all_barrier(gx, gy, me_x, me_y)
    rows = (lambda i: send.at[i], lambda i: got.at[i], sem_a, sem_b, local.at[0])
    tallies = (lambda i: tally.at[i], lambda i: got_tally.at[i], sem_c, sem_d, local.at[1])
    end_x = exchange(me_x, gx, [rows, tallies], lambda i: (i, me_y))
    others = (lambda i: small.at[i], lambda i: got_small.at[i], sem_e, sem_f, local.at[2])
    end_all = exchange(
        me_x * gy + me_y, gx * gy, [others], lambda i: (i // gy, lax.rem(i, gy))
    )
    end_x()
    end_all()


def to_ranges(gx, gy, send, tally, got, got_tally, sem_a, sem_b, sem_c, sem_d, local):
    me_x, me_y = lax.axis_index("gx"), lax.axis_index("gy")
    all_barrier(gx, gy, me_x, me_y)
    rows = (
        lambda i: send.at[lax.rem(i, gy) * gx + i // gy],
        lambda i: got.at[i],
        sem_a,
        sem_b,
        local.at[0],
    )
    end_all = exchange(
        me_x * gy + me_y, gx * gy, [rows], lambda i: (i // gy, lax.rem(i, gy))
    )
    tallies = (lambda i: tally.at[i], lambda i: got_tally.at[i], sem_c, sem_d, local.at[1])
    end_y = exchange(me_y, gy, [tallies], lambda i: (me_x, i))
    end_y()
    end_all()


def shaped(*dims, dtype=F32):
    return jax.ShapeDtypeStruct(dims, dtype)


def body(measures, row_keys, orders, heavy_keys, key_slot):
    rows, columns = measures.shape
    gx, gy = lax.axis_size("gx"), lax.axis_size("gy")
    devices = gx * gy
    key_dev = orders.shape[0]
    key_rows = key_dev // LANES
    own = key_dev * gy
    nr = key_slot.shape[0] // LANES
    heavy = heavy_keys.shape[0]
    each = heavy // devices
    capacity = max(rows // 32, 3 * rows // (4 * gx)) // 4
    segments = gx * capacity
    cfg = dict(
        rows=rows,
        block=min(rows, 2048),
        nr=nr,
        gx=gx,
        gy=gy,
        devices=devices,
        own=own,
        kpp=key_dev // gx,
        key_rows=key_rows,
        heavy=heavy,
        heavy_each=each,
        height=-(-(each + key_rows) // 8) * 8,
        capacity=capacity,
        segments=segments,
        seg_block=512 if segments % 512 == 0 else segments,
    )
    height = cfg["height"]
    group = own // LANES
    params = pltpu.CompilerParams(vmem_limit_bytes=LIMIT)
    table = key_slot.reshape(nr, LANES)
    send, tally, small = pl.pallas_call(
        functools.partial(gather_rows, cfg),
        out_shape=(
            shaped(segments, columns),
            shaped(nr, LANES),
            shaped(devices * height, LANES),
        ),
        in_specs=[VMEM] * 4,
        out_specs=(VMEM,) * 3,
        scratch_shapes=[pltpu.VMEM((1, rows), jnp.int32)],
        compiler_params=params,
    )(measures, row_keys.reshape(1, rows), heavy_keys.reshape(heavy, 1), table)
    dma = pltpu.SemaphoreType.DMA
    got, got_tally, got_small = pl.pallas_call(
        functools.partial(to_owners, gx, gy),
        out_shape=(
            shaped(gx, capacity, columns),
            shaped(gx, group, LANES),
            shaped(devices, height, LANES),
        ),
        in_specs=[ANY] * 3,
        out_specs=(ANY,) * 3,
        scratch_shapes=[dma((gx,))] * 4 + [dma((devices,))] * 2 + [dma((3,))],
        compiler_params=pltpu.CompilerParams(collective_id=0, has_side_effects=True),
    )(
        send.reshape(gx, capacity, columns),
        tally.reshape(gx, group, LANES),
        small.reshape(devices, height, LANES),
    )
    send2, tally2 = pl.pallas_call(
        functools.partial(place_rows, cfg),
        out_shape=(shaped(own, columns), shaped(group, LANES)),
        in_specs=[VMEM] * 3,
        out_specs=(VMEM,) * 2,
        scratch_shapes=[pltpu.VMEM((own, LANES), F32), pltpu.VMEM((gx * group, LANES), F32)],
        compiler_params=params,
    )(got.reshape(segments, columns), got_tally.reshape(gx * group, LANES), table)
    got2, got_tally2 = pl.pallas_call(
        functools.partial(to_ranges, gx, gy),
        out_shape=(shaped(devices, cfg["kpp"], columns), shaped(gy, key_rows, LANES)),
        in_specs=[ANY] * 2,
        out_specs=(ANY,) * 2,
        scratch_shapes=[dma((devices,))] * 2 + [dma((gy,))] * 2 + [dma((2,))],
        compiler_params=pltpu.CompilerParams(collective_id=1, has_side_effects=True),
    )(send2.reshape(devices, cfg["kpp"], columns), tally2.reshape(gy, key_rows, LANES))
    result, report, slot_rows = pl.pallas_call(
        functools.partial(join_rows, cfg),
        out_shape=(
            shaped(key_dev, columns, dtype=BF16),
            shaped(each, columns, dtype=BF16),
            shaped(key_rows, LANES),
        ),
        in_specs=[SMEM] + [VMEM] * 5,
        out_specs=(VMEM,) * 3,
        scratch_shapes=[pltpu.VMEM((key_dev, LANES), F32)] * 2,
        compiler_params=params,
    )(
        heavy_keys,
        got2.reshape(devices * cfg["kpp"], columns),
        got_small.reshape(devices * height, LANES),
        got_tally2.reshape(gy * key_rows, LANES),
        orders,
        table,
    )
    return (result, report, slot_rows.reshape(key_dev))


def solution(mesh):
    return jax.shard_map(
        body,
        mesh=mesh,
        in_specs=(P(("gx", "gy"), None), P(("gx", "gy")), P(("gx", "gy"), None), P(), P()),
        out_specs=(P(("gx", "gy"), None), P(("gx", "gy"), None), P(("gx", "gy"))),
        check_vma=False,
    )
```

time: 409 us -> 87 us (0.21); the launches traced: 402 us -> 86.8 us
  local copies, waits for them, and re-layouts: 170 us -> 1.36 us
  blocking collectives: 85.8 us -> 0 us
  Pallas kernels: 0 us -> 84.8 us
  other arithmetic: 51.7 us -> 0 us
  matrix products: 35 us -> 0 us
  starting transfers between devices: 26.8 us -> 0 us
  waiting for transfers between devices: 18.1 us -> 0 us
  between operations: 14.3 us -> 0.65 us
    gather x8 -> x0, local copies, waits for them, and re-layouts: 103 us -> none  [the longest x1 45.5 us: body(): slot_ids = key_slot[row_keys]]
    pallas_call x0 -> x5, Pallas kernels: none -> 84.8 us  [the longest x1 29.5 us: body(): pl.pallas_call(functools.partial(to_ranges, gx, gy), out_shape=(shaped(de...]
    scatter x2 -> x0, local copies, waits for them, and re-layouts: 61.1 us -> none  [the longest x1 30.7 us: body(): row_segment = jnp.zeros((row_count,), jnp.int32).at[ordering].set(segment)]
    psum x1 -> x0, blocking collectives: 49.8 us -> none  [body(): joined_total, count_total = lax.psum((joined, heavy_count), ('gx', 'gy'))]
    dot_general x9 -> x0, matrix products: 35 us -> none  [the longest x8 28.7 us: add_block(): lax.dot_general(onehot, block_values, (((0,), (0,)), ((), ())), preferred...]
    all_gather x1 -> x0, blocking collectives: 29.6 us -> none  [body(): lax.all_gather(heavy_orders_here, ('gx', 'gy'), axis=0, tiled=True)]
    all_to_all x5 -> x0, starting transfers between devices: 26.8 us -> none  [the longest x1 6.35 us: body(): lax.all_to_all(tallies.reshape(groups_x, key_capacity), 'gx', split_axis=...]
    sort x5 -> x0, other arithmetic: 25.8 us -> none  [the longest x1 7.75 us: body(): inverse = jnp.argsort(key_slot)]
  transfers between devices with their start and end apart: 6 -> 0, of which waited for: 3 -> 0; matrix products, arithmetic and copies ran while one was open for 24% -> 0% of each run, Pallas kernels for 0% -> 0%
where the time goes in v1:
time: 87 us; the launch traced here: 86.8 us
  Pallas kernels  84.8 us (97%)
  local copies, waits for them, and re-layouts  1.36 us (2%)
    pallas_call x1, Pallas kernels, body(): pl.pallas_call(functools.partial(to_ranges, gx, gy), out_shape=(shaped(de...  29.5 us
    pallas_call x1, Pallas kernels, body(): pl.pallas_call(functools.partial(to_owners, gx, gy), out_shape=(shaped(gx...  29 us
    pallas_call x1, Pallas kernels, body(): pl.pallas_call(functools.partial(gather_rows, cfg), out_shape=(shaped(seg...  16.2 us
    pallas_call x1, Pallas kernels, body(): pl.pallas_call(functools.partial(place_rows, cfg), out_shape=(shaped(own,...  7.29 us
    pallas_call x1, Pallas kernels, body(): pl.pallas_call(functools.partial(join_rows, cfg), out_shape=(shaped(key_d...  2.79 us

profile of v1, /device:TPU:15, one launch (start us, length us, event | category | flops | bytes accessed | tf_op | source)
XLA Modules:
  0.0 86.8 jit_solution(10799277476026214865)
XLA Ops:
  0.6 1.4 %copy.8.heavy = s32[64,1]{1,0:T(8,128)} copy(s32[64,1]{0,1:T(1,128)} %bitcast.28) | data formatting | bytes 512 | tf_op jit(solution)/shard_map/reshape | solution.py:353
  2.0 16.2 %shard_map.76 = (f32[1536,128]{1,0:T(8,128)}, f32[128,128]{1,0:T(8,128)}, f32[256,128]{1,0:T(8,128)}) custom-call(bf16[8192,128]{1,0:T(8,128)(2,1)} %measures.1, s32[1,8192]{1,0:T(1,128)} %bitcast.25, s32[64,1]{1,0:T(8,128)} %copy.8.heavy, s32[128,128]{1,0:T(8,128)} %bitcast.18), custom_call_target="tpu_custom_call" | custom-call | tf_op jit(solution)/shard_map/pallas_call | solution.py:342
  18.2 29.0 %shard_map.77 = (f32[8,192,128]{2,1,0:T(8,128)}, f32[8,16,128]{2,1,0:T(8,128)}, f32[32,8,128]{2,1,0:T(8,128)}) custom-call(f32[8,192,128]{2,1,0:T(8,128)} %bitcast.17, f32[8,16,128]{2,1,0:T(8,128)} %bitcast.24, f32[32,8,128]{2,1,0:T(8,128)} %bitcast.22), custom_call_target="tpu_custom_call" | custom-call | tf_op jit(solution)/shard_map/pallas_call | solution.py:355
  47.2 7.3 %shard_map.78 = (f32[2048,128]{1,0:T(8,128)}, f32[16,128]{1,0:T(8,128)}) custom-call(f32[1536,128]{1,0:T(8,128)} %bitcast.16, f32[128,128]{1,0:T(8,128)} %bitcast.23, s32[128,128]{1,0:T(8,128)} %bitcast.19), custom_call_target="tpu_custom_call" | custom-call | tf_op jit(solution)/shard_map/pallas_call | solution.py:371
  54.5 29.5 %shard_map.79 = (f32[32,64,128]{2,1,0:T(8,128)}, f32[4,4,128]{2,1,0:T(4,128)}) custom-call(f32[32,64,128]{2,1,0:T(8,128)} %bitcast.15, f32[4,4,128]{2,1,0:T(4,128)} %bitcast.27), custom_call_target="tpu_custom_call" | custom-call | tf_op jit(solution)/shard_map/pallas_call | solution.py:379
  84.0 2.8 %shard_map.80 = (bf16[512,128]{1,0:T(8,128)(2,1)}, bf16[2,128]{1,0:T(2,128)(2,1)}, f32[4,128]{1,0:T(4,128)}) custom-call(s32[64]{0:T(128)} %heavy.1, f32[2048,128]{1,0:T(8,128)} %bitcast.14, f32[256,128]{1,0:T(8,128)} %bitcast.21, f32[16,128]{1,0:T(8,128)} %bitcast.26, bf16[512,128]{1,0:T(8,128)(2,1)} %orders.1, s32[128,128]{1,0:T(8,128)} %bitcast.20), custom_call_target="tpu_custom_call" | custom-call | tf_op jit(solution)/shard_map/pallas_call | solution.py:387
